TPU v7x, 32 devices: a whole 2x2x4 slice. The times are simulated.
32 devices in a mesh: groups: 2 (over y), tok: 8 (over z, core), head: 2 (over x), pair: 1.
Axes of the slice: x: 2, y: 2, z: 4, core: 2. Of those that a mesh axis runs over, the one named last changes fastest.
Arguments:
- queries: bfloat16 [2048, 4096], P(('groups', 'tok'), ('head', 'pair')), parts along dimension 0, may hold values from -6 to 6
- keys_values: bfloat16 [2048, 1024], P(('groups', 'tok'), ('head', 'pair')), parts along dimension 0, may hold values from -6 to 6
- sink_logits: float32 [64], P(('head', 'pair')), may hold values from -2 to 3
- residual: bfloat16 [2048, 2880], P(('groups', 'tok')), parts along dimension 0, may hold values from -60 to 60
- out_weight: bfloat16 [4096, 2880], P(('head', 'pair')), may hold values from -0.09375 to 0.09375
- norm_gain: float32 [2880], replicated, may hold values from 0.5 to 1.5
- expert_ids: int32 [2048, 4], P(('groups', 'tok')), parts along dimension 0, may hold values from 0 to 7, all different within a row; in each aligned block of 128 rows (0 to 127, 128 to 255, ...) at most 80 rows name the same one
- route_weights: float32 [2048, 4], P(('groups', 'tok')), parts along dimension 0, may hold values from 0.1 to 1
- gate_up: bfloat16 [8, 2880, 2, 1440], P('tok', None, None, ('head', 'pair')), may hold values from -0.109375 to 0.109375
- down_weight: bfloat16 [8, 1440, 2880], P('tok', ('head', 'pair')), may hold values from -0.21875 to 0.21875
Outputs:
- layer_output: bfloat16 [2048, 2880], P(('groups', 'tok'), ('head', 'pair')), parts along dimension 0
There are 2 independent parts, one for each index of `groups`. A program takes and returns all parts, laid end to end along the dimension named above; an argument that names none is the same for every part. Nothing has to cross between parts.
Inputs may be any that keep to these rules, and one draw needn't show every extreme that they name: `expert_ids`: in each aligned block of 128 rows (the rows of one index of tok), a row names 4 different experts and no expert is named by more than 80 rows.
All inputs are finite; a program needn't handle non-finite values.
Results may differ from a plain program's by a relative error of at most 0.01.
Values may be sent and summed in bfloat16 or wider, within the bound.
A program may use at most 128 MiB of HBM per device.

v0:
```python
import jax
import jax.numpy as jnp
from jax import lax
from jax.sharding import PartitionSpec as P

HEAD_DIM = 64


def slot_places(expert_ids, experts, capacity):
    tok_rows = expert_ids.shape[0]
    fanout = expert_ids.shape[1]
    flat_ids = expert_ids.reshape(-1)
    one_hot = (flat_ids[:, None] == jnp.arange(experts, dtype=jnp.int32)[None, :]).astype(jnp.int32)
    earlier = jnp.cumsum(one_hot, axis=0) - one_hot
    ranking = jnp.sum(earlier * one_hot, axis=1)
    targets = flat_ids * capacity + ranking
    sources = jnp.arange(tok_rows * fanout, dtype=jnp.int32) // fanout
    table = jnp.full((experts * capacity,), tok_rows, jnp.int32).at[targets].set(sources)
    return (targets.reshape(tok_rows, fanout), table)


def active_rows(flat_rows, gate_up):
    local_hidden = gate_up.shape[-1]
    both_columns = gate_up.reshape(flat_rows.shape[-1], 2 * local_hidden)
    both = jnp.dot(flat_rows, both_columns, preferred_element_type=jnp.float32)
    gate_part = both[:, :local_hidden]
    up_part = both[:, local_hidden:]
    return (gate_part * jax.nn.sigmoid(1.702 * gate_part) * (up_part + 1.0)).astype(jnp.bfloat16)


def per_device(
    queries,
    keys_values,
    sink_logits,
    residual,
    out_weight,
    norm_gain,
    expert_ids,
    route_weights,
    gate_up,
    down_weight,
):
    tok_rows = queries.shape[0]
    kv_groups = keys_values.shape[1] // (2 * HEAD_DIM)
    local_heads = queries.shape[1] // HEAD_DIM
    repeat = local_heads // kv_groups
    position = lax.axis_index("tok") * tok_rows + jnp.arange(tok_rows, dtype=jnp.int32)
    grouped = queries.reshape(tok_rows, kv_groups, repeat, HEAD_DIM)
    start_max = jnp.broadcast_to(
        sink_logits.reshape(kv_groups, repeat)[:, :, None], (kv_groups, repeat, tok_rows)
    )
    start_totals = jnp.ones((kv_groups, repeat, tok_rows), jnp.float32)
    start_accum = jnp.zeros((kv_groups, repeat, tok_rows, HEAD_DIM), jnp.float32)
    key_piece = lax.all_gather(keys_values, "tok", axis=0, tiled=True)
    totals = start_totals
    accum = start_accum
    count = key_piece.shape[0]
    split_piece = key_piece.reshape(count, kv_groups, 2, HEAD_DIM)
    scores = (
        jnp.einsum(
            "tgrd,ngd->grtn", grouped, split_piece[:, :, 0], preferred_element_type=jnp.float32
        )
        * 0.125
    )
    key_position = jnp.arange(count, dtype=jnp.int32)
    allowed = key_position[None, :] <= position[:, None]
    scores = jnp.where(allowed, scores, jnp.float32(-1e30))
    new_max = jnp.maximum(start_max, jnp.max(scores, axis=-1))
    decay = jnp.exp(start_max - new_max)
    weights = jnp.exp(scores - new_max[..., None])
    totals = totals * decay + jnp.sum(weights, axis=-1)
    update = jnp.einsum(
        "grtn,ngd->grtd",
        weights.astype(jnp.bfloat16),
        split_piece[:, :, 1],
        preferred_element_type=jnp.float32,
    )
    accum = accum * decay[..., None] + update
    final_max, totals, accum = (new_max, totals, accum)
    attended = (accum / totals[..., None]).astype(jnp.bfloat16)
    attended = jnp.transpose(attended, (2, 0, 1, 3)).reshape(tok_rows, local_heads * HEAD_DIM)
    width = out_weight.shape[1]
    experts = lax.axis_size("tok")
    fanout = expert_ids.shape[1]
    capacity = min(tok_rows, tok_rows * fanout * 5 // (4 * experts))
    targets, table = slot_places(expert_ids, experts, capacity)
    share = width // lax.axis_size(("head", "pair"))
    column_start = lax.axis_index(("head", "pair")) * share
    partial_value = jnp.dot(attended, out_weight, preferred_element_type=jnp.float32)
    projected = lax.psum(partial_value.astype(jnp.bfloat16), ("head", "pair")).astype(jnp.float32)
    stream = residual.astype(jnp.float32) + projected
    inverse = lax.rsqrt(jnp.mean(stream * stream, axis=-1, keepdims=True) + 1e-05)
    normed = (stream * inverse * norm_gain).astype(jnp.bfloat16)
    padded = jnp.concatenate([normed, jnp.zeros((1, width), jnp.bfloat16)], axis=0)
    outgoing = padded[table].reshape(experts, capacity, width)
    received = lax.all_to_all(outgoing, "tok", split_axis=0, concat_axis=0, tiled=True)
    shape_in = received.shape
    active = active_rows(received.reshape(-1, shape_in[-1]), gate_up)
    partial_value = jnp.dot(active, down_weight[0], preferred_element_type=jnp.float32)
    partial_out = partial_value.reshape(shape_in[:-1] + (partial_value.shape[-1],))
    stream_share = lax.dynamic_slice_in_dim(stream, column_start, share, 1)
    expert_out = lax.psum_scatter(
        partial_out.astype(jnp.bfloat16), ("head", "pair"), scatter_dimension=2, tiled=True
    )
    returned = lax.all_to_all(expert_out, "tok", split_axis=0, concat_axis=0, tiled=True)
    flat_out = returned.reshape(experts * capacity, share)
    picked = flat_out[targets]
    mixture = jnp.sum(route_weights[:, :, None] * picked.astype(jnp.float32), axis=1)
    return (stream_share + mixture).astype(jnp.bfloat16)


def solution(mesh):
    placed = (
        P(("groups", "tok"), ("head", "pair")),
        P(("groups", "tok"), ("head", "pair")),
        P(("head", "pair")),
        P(("groups", "tok"), None),
        P(("head", "pair"), None),
        P(),
        P(("groups", "tok"), None),
        P(("groups", "tok"), None),
        P("tok", None, None, ("head", "pair")),
        P("tok", ("head", "pair"), None),
    )
    return jax.shard_map(
        per_device,
        mesh=mesh,
        in_specs=placed,
        out_specs=P(("groups", "tok"), ("head", "pair")),
        check_vma=False,
    )
```

profile of v0, /device:TPU:0, one launch (start us, length us, event | category | flops | bytes accessed | tf_op | source)
XLA Modules:
  0.0 360.1 jit_solution(5080762425905200024)
XLA Ops:
  6.5 0.0 all-gather.2.cloned.1.call-start
  6.5 1.7 copy.27
  8.2 0.0 all-gather.2.cloned.1.call-update
  8.2 0.0 all-reduce.3.cloned.1.call-start
  8.3 0.8 copy.33
  9.1 0.1 eq.29
  9.2 0.1 eq.25
  9.3 1.3 copy.29
  10.6 0.7 broadcast_in_dim.20
  11.4 1.1 reduce-window.6
  12.5 0.2 slice_reduce_fusion
  12.8 0.1 fusion.19
  12.8 0.1 reduce_sum.44
  13.0 0.1 iota_compare_fusion
  13.1 22.5 %all-gather.2.cloned.1.call-done = bf16[1024,512]{0,1:T(8,128)(2,1)} async-done(((bf16[128,512]{0,1:T(8,128)(2,1)}), bf16[1024,512]{0,1:T(8,128)(2,1)}) %all-gather.2.cloned.1.call-update) | async-done | bytes 1048592 | tf_op jit(solution)/shard_map/all_gather | solution.py:54
  35.6 8.1 %fusion.2 = (f32[4,8,128]{2,1,0:T(8,128)S(1)}, f32[4,1024,128,8]{2,1,3,0:T(8,128)}) fusion(pred[128,1024]{0,1:T(8,128)(4,1)S(1)} %iota_compare_fusion, bf16[128,4,8,64]{0,3,2,1:T(8,128)(2,1)S(1)} %bitcast.78, bf16[1024,4,2,64]{0,3,2,1:T(8,128)(2,1)} %bitcast.80), kind=kOutput, calls=%fused_computation.7 | convolution fusion | flops 549449728 | bytes 17973248 | tf_op jit(solution)/shard_map/tgrd,ngd->grtn/dot_general | solution.py:60
  43.6 0.1 broadcast_maximum_fusion
  43.7 0.0 copy-start.1
  43.7 9.3 %fusion = f32[4,8,128]{2,1,0:T(8,128)S(1)} fusion(f32[4,1024,128,8]{2,1,3,0:T(8,128)} %get-tuple-element.12, f32[4,8,128]{2,1,0:T(8,128)S(1)} %broadcast_maximum_fusion, pred[128,1024]{0,1:T(8,128)(4,1)S(1)} %iota_compare_fusion), kind=kLoop, calls=%fused_computation.5 | loop fusion | flops 16773120 | bytes 16941056 | tf_op jit(solution)/shard_map/reduce_sum | solution.py:71
  53.0 0.1 multiply_bitcast_fusion
  53.1 0.0 copy-done.1
  53.1 7.8 %divide_convert_fusion = bf16[128,4,8,64]{0,3,2,1:T(8,128)(2,1)S(1)} fusion(f32[4,1024,128,8]{2,1,3,0:T(8,128)} %get-tuple-element.12, f32[4,8,128]{2,1,0:T(8,128)S(1)} %broadcast_maximum_fusion, pred[128,1024]{0,1:T(8,128)(4,1)S(1)} %iota_compare_fusion, bf16[1024,4,2,64]{0,3,2,1:T(8,128)(2,1)S(1)} %bitcast.81, f32[128,4,8]{0,2,1:T(8,128)S(1)} %get-tuple-element.10, ...), kind=kOutput, calls=%fused_computation.22 | convolution fusion | flops 554434560 | bytes 18006016 | tf_op jit(solution)/shard_map/grtn,ngd->grtd/dot_general | solution.py:72
  60.9 0.0 copy-start
  60.9 7.1 %convolution_convert_fusion.1 = bf16[128,2880]{0,1:T(8,128)(2,1)} fusion(bf16[2048,2880]{0,1:T(8,128)(2,1)} %param.14, bf16[128,2048]{0,1:T(8,128)(2,1)S(1)} %bitcast.85), kind=kOutput, calls=%fused_computation.12 | convolution fusion | flops 1510318080 | bytes 13058048 | tf_op jit(solution)/shard_map/dot_general | solution.py:89
  68.0 0.0 copy-start.2
  68.0 0.0 all-reduce.3.cloned.1.call-update
  68.0 0.0 reduce-scatter.4.cloned.1.call-start
  68.1 0.1 mul.93
  68.2 2.6 scatter_custom_fusion
  70.9 29.3 %all-reduce.3.cloned.1.call-done = bf16[128,2880]{0,1:T(8,128)(2,1)} async-done(((bf16[128,2880]{0,1:T(8,128)(2,1)}), bf16[128,2880]{0,1:T(8,128)(2,1)}) %all-reduce.3.cloned.1.call-update) | async-done | bytes 737296 | tf_op jit(solution)/shard_map/psum | solution.py:90
  100.2 0.0 copy-done
  100.2 2.6 convert_add_fusion
  102.8 0.0 copy-done.2
  102.8 1.6 multiply_convert_fusion
  104.4 0.3 copy.46
  104.7 0.1 concatenate.3.clone
  104.8 4.6 %gather_fusion = bf16[640,2880]{1,0:T(8,128)(2,1)} fusion(bf16[129,2880]{1,0:T(8,128)(2,1)S(1)} %concatenate.3.clone, s32[1024]{0:T(1024)S(1)} %pad_clamp_fusion.1), kind=kCustom, calls=%fused_computation | custom fusion | bytes 7375360 | tf_op jit(solution)/shard_map/gather | solution.py:95
  109.4 89.4 %all_to_all.10 = bf16[8,80,2880]{2,1,0:T(8,128)(2,1)S(1)} all-to-all(bf16[8,80,2880]{2,1,0:T(8,128)(2,1)} %bitcast.75), channel_id=1, replica_groups=mesh['groups'=2,'tok'=8,'head'=2,'pair'=1] {'tok'}, dimensions={0} | all-to-all | bytes 7372800 | tf_op jit(solution)/shard_map/all_to_all | solution.py:96
  198.8 9.5 %fusion.28 = f32[640,1440]{0,1:T(8,128)S(1)} fusion(bf16[640,2880]{1,0:T(8,128)(2,1)S(1)} %bitcast.77, bf16[2880,1440]{0,1:T(8,128)(2,1)} %bitcast.84), kind=kOutput, calls=%fused_computation.58 | convolution fusion | flops 5308416000 | bytes 15667200 | tf_op jit(solution)/shard_map/dot_general | solution.py:25
  208.3 0.5 fusion.8
  208.8 1.0 copy.37
  209.9 7.0 %convolution_convert_fusion = bf16[8,80,2880]{2,1,0:T(8,128)(2,1)} fusion(bf16[8,80,720]{2,1,0:T(8,128)(2,1)S(1)} %bitcast.79, bf16[1,720,2880]{2,1,0:T(8,128)(2,1)} %param.19), kind=kOutput, calls=%fused_computation.10 | convolution fusion | flops 2656051200 | bytes 8755200 | tf_op jit(solution)/shard_map/dot_general | solution.py:99
  216.9 8.1 %copy.42 = bf16[8,80,2880]{1,0,2:T(8,128)(2,1)} copy(bf16[8,80,2880]{2,1,0:T(8,128)(2,1)} %convolution_convert_fusion) | data formatting | bytes 7372800
  225.0 9.6 %reshape.137 = bf16[2880,640]{1,0:T(8,128)(2,1)} reshape(bf16[2880,8,80]{2,1,0:T(8,128)(2,1)} %bitcast.74) | data formatting | bytes 7372800
  234.6 0.0 reduce-scatter.4.cloned.1.call-update
  234.6 47.5 %reduce-scatter.4.cloned.1.call-done = bf16[1440,640]{1,0:T(8,128)(2,1)} async-done(((bf16[2880,640]{1,0:T(8,128)(2,1)}), bf16[1440,640]{1,0:T(8,128)(2,1)}) %reduce-scatter.4.cloned.1.call-update) | async-done | bytes 1843216
  282.1 4.8 %reshape.138 = bf16[1440,8,80]{2,1,0:T(8,128)(2,1)S(1)} reshape(bf16[1440,640]{1,0:T(8,128)(2,1)} %reduce-scatter.4.cloned.1.call-done) | data formatting | bytes 3686400
  286.9 0.0 copy-start.3
  286.9 3.5 copy.43
  290.5 4.6 %all-to-all-start.1 = ((bf16[8,80,1440]{2,1,0:T(8,128)(2,1)}), bf16[8,80,1440]{2,1,0:T(8,128)(2,1)S(1)}, u32[]{:S(2)}, u32[]{:S(2)}) async-start(bf16[8,80,1440]{2,1,0:T(8,128)(2,1)} %copy.43), calls=%async_computation.1 | async-start | bytes 3932160 | tf_op jit(solution)/shard_map/all_to_all | solution.py:105
  295.1 0.1 reshape.116
  295.2 0.0 copy-done.3
  295.2 0.1 copy.32
  295.3 46.0 %all-to-all-done.1 = bf16[8,80,1440]{2,1,0:T(8,128)(2,1)S(1)} async-done(((bf16[8,80,1440]{2,1,0:T(8,128)(2,1)}), bf16[8,80,1440]{2,1,0:T(8,128)(2,1)S(1)}, u32[]{:S(2)}, u32[]{:S(2)}) %all-to-all-start.1) | async-done | bytes 1843232 | tf_op jit(solution)/shard_map/all_to_all | solution.py:105
  341.3 3.0 gather_fusion.1
  344.2 2.9 reshape.133
  347.2 3.1 multiply_reduce_fusion
  350.2 1.4 copy.38
  351.6 1.9 add_convert_fusion
  (11 shorter events, 0.1 us)
Async XLA Ops:
  6.5 29.0 %all-gather.2.cloned.1.call-start = ((), (), s32[]{:S(2)}) async-start(), calls=%async_computation.3 | async-start | bytes 1179648 | tf_op jit(solution)/shard_map/all_gather | solution.py:54
  8.2 92.0 %all-reduce.3.cloned.1.call-start = ((), (), s32[]{:S(2)}) async-start(), calls=%async_computation.4 | async-start | bytes 1474560 | tf_op jit(solution)/shard_map/psum | solution.py:90
  43.7 9.3 %copy-start.1 = (bf16[1024,512]{0,1:T(8,128)(2,1)S(1)}, bf16[1024,512]{0,1:T(8,128)(2,1)}, u32[]{:S(2)}) copy-start(bf16[1024,512]{0,1:T(8,128)(2,1)} %all-gather.2.cloned.1.call-done) | copy-start | bytes 3145732
  60.9 39.3 %copy-start = (bf16[128,2880]{0,1:T(8,128)(2,1)S(1)}, bf16[128,2880]{0,1:T(8,128)(2,1)}, u32[]{:S(2)}) copy-start(bf16[128,2880]{0,1:T(8,128)(2,1)} %param.13) | copy-start | bytes 2211844
  68.0 34.8 %copy-start.2 = (f32[2880]{0:T(1024)S(1)}, f32[2880]{0:T(1024)}, u32[]{:S(2)}) copy-start(f32[2880]{0:T(1024)} %param.15) | copy-start | bytes 34564
  68.0 214.1 %reduce-scatter.4.cloned.1.call-start = ((), (), s32[]{:S(2)}) async-start(), calls=%async_computation.5 | async-start | bytes 5529600
  286.9 8.3 %copy-start.3 = (f32[128,4]{0,1:T(4,128)S(1)}, f32[128,4]{0,1:T(4,128)}, u32[]{:S(2)}) copy-start(f32[128,4]{0,1:T(4,128)} %param.17) | copy-start | bytes 6148
  290.5 50.8 %all-to-all-start.1 = ((bf16[8,80,1440]{2,1,0:T(8,128)(2,1)}), bf16[8,80,1440]{2,1,0:T(8,128)(2,1)S(1)}, u32[]{:S(2)}, u32[]{:S(2)}) async-start(bf16[8,80,1440]{2,1,0:T(8,128)(2,1)} %copy.43), calls=%async_computation.1 | async-start | bytes 3932160 | tf_op jit(solution)/shard_map/all_to_all | solution.py:105
Sparse Core Ops, SparseCore 0:
  8.9 26.5 all-gather.1
  68.1 32.0 all-reduce.2
  234.7 47.3 reduce-scatter.3
where the time goes:
time: 361 us; the launch traced here: 360 us
  waiting for transfers between devices  145 us (40%)
  blocking collectives  89.4 us (25%)
  local copies, waits for them, and re-layouts  47.4 us (13%)
  matrix products  39.4 us (11%)
  other arithmetic  20.5 us (6%)
  between operations  13.3 us (4%)
  starting transfers between devices  4.69 us (1%)
    all_to_all x1, blocking collectives, per_device(): lax.all_to_all(outgoing, 'tok', split_axis=0, concat_axis=0, tiled=True)  89.4 us
    unnamed x4, waiting for transfers between devices  47.5 us
    all_to_all x1, waiting for transfers between devices, per_device(): lax.all_to_all(expert_out, 'tok', split_axis=0, concat_axis=0, tiled=True)  46 us
    unnamed x17, local copies, waits for them, and re-layouts  30.3 us
    psum x1, waiting for transfers between devices, per_device(): lax.psum(partial_value.astype(jnp.bfloat16), ('head', 'pair'))  29.3 us
    all_gather x1, waiting for transfers between devices, per_device(): key_piece = lax.all_gather(keys_values, 'tok', axis=0, tiled=True)  22.5 us
    dot_general x1, matrix products, active_rows(): both = jnp.dot(flat_rows, both_columns, preferred_element_type=jnp.float32)  9.46 us
    reduce_sum x1, other arithmetic, per_device(): totals = totals * decay + jnp.sum(weights, axis=-1)  9.26 us
  transfers between devices with their start and end apart: 4, of which 4 were waited for; matrix products, arithmetic and copies ran while one was open for 2% of the time, Pallas kernels for 0%

commit v1 on v0

--- a/solution.py
+++ b/solution.py
@@ -87,7 +87,9 @@
     share = width // lax.axis_size(("head", "pair"))
     column_start = lax.axis_index(("head", "pair")) * share
     partial_value = jnp.dot(attended, out_weight, preferred_element_type=jnp.float32)
-    projected = lax.psum(partial_value.astype(jnp.bfloat16), ("head", "pair")).astype(jnp.float32)
+    projected = lax.psum(lax.psum(partial_value.astype(jnp.bfloat16), "pair"), "head").astype(
+        jnp.float32
+    )
     stream = residual.astype(jnp.float32) + projected
     inverse = lax.rsqrt(jnp.mean(stream * stream, axis=-1, keepdims=True) + 1e-05)
     normed = (stream * inverse * norm_gain).astype(jnp.bfloat16)

time: 361 us -> 361 us (level)
  no operation moved by 1% of the time
where the time goes in v1:
time: 361 us; the launch traced here: 360 us
  waiting for transfers between devices  145 us (40%)
  blocking collectives  89.4 us (25%)
  local copies, waits for them, and re-layouts  47.4 us (13%)
  matrix products  39.4 us (11%)
  other arithmetic  20.5 us (6%)
  between operations  13.3 us (4%)
  starting transfers between devices  4.69 us (1%)
    all_to_all x1, blocking collectives, per_device(): lax.all_to_all(outgoing, 'tok', split_axis=0, concat_axis=0, tiled=True)  89.4 us
    unnamed x4, waiting for transfers between devices  47.5 us
    all_to_all x1, waiting for transfers between devices, per_device(): lax.all_to_all(expert_out, 'tok', split_axis=0, concat_axis=0, tiled=True)  46 us
    unnamed x17, local copies, waits for them, and re-layouts  30.3 us
    psum x1, waiting for transfers between devices, per_device(): lax.psum(lax.psum(partial_value.astype(jnp.bfloat16), 'pair'), 'head')  29.3 us
    all_gather x1, waiting for transfers between devices, per_device(): key_piece = lax.all_gather(keys_values, 'tok', axis=0, tiled=True)  22.5 us
    dot_general x1, matrix products, active_rows(): both = jnp.dot(flat_rows, both_columns, preferred_element_type=jnp.float32)  9.46 us
    reduce_sum x1, other arithmetic, per_device(): totals = totals * decay + jnp.sum(weights, axis=-1)  9.26 us
  transfers between devices with their start and end apart: 4, of which 4 were waited for; matrix products, arithmetic and copies ran while one was open for 2% of the time, Pallas kernels for 0%

profile of v1, /device:TPU:0, one launch (start us, length us, event | category | flops | bytes accessed | tf_op | source)
XLA Modules:
  0.0 360.1 jit_solution(5080762425905200024)
XLA Ops:
  6.5 0.0 all-gather.2.cloned.1.call-start
  6.5 1.7 copy.27
  8.2 0.0 all-gather.2.cloned.1.call-update
  8.2 0.0 all-reduce.3.cloned.1.call-start
  8.3 0.8 copy.33
  9.1 0.1 eq.29
  9.2 0.1 eq.25
  9.3 1.3 copy.29
  10.6 0.7 broadcast_in_dim.20
  11.4 1.1 reduce-window.6
  12.5 0.2 slice_reduce_fusion
  12.8 0.1 fusion.19
  12.8 0.1 reduce_sum.44
  13.0 0.1 iota_compare_fusion
  13.1 22.5 %all-gather.2.cloned.1.call-done = bf16[1024,512]{0,1:T(8,128)(2,1)} async-done(((bf16[128,512]{0,1:T(8,128)(2,1)}), bf16[1024,512]{0,1:T(8,128)(2,1)}) %all-gather.2.cloned.1.call-update) | async-done | bytes 1048592 | tf_op jit(solution)/shard_map/all_gather | solution.py:54
  35.6 8.1 %fusion.2 = (f32[4,8,128]{2,1,0:T(8,128)S(1)}, f32[4,1024,128,8]{2,1,3,0:T(8,128)}) fusion(pred[128,1024]{0,1:T(8,128)(4,1)S(1)} %iota_compare_fusion, bf16[128,4,8,64]{0,3,2,1:T(8,128)(2,1)S(1)} %bitcast.78, bf16[1024,4,2,64]{0,3,2,1:T(8,128)(2,1)} %bitcast.80), kind=kOutput, calls=%fused_computation.7 | convolution fusion | flops 549449728 | bytes 17973248 | tf_op jit(solution)/shard_map/tgrd,ngd->grtn/dot_general | solution.py:60
  43.6 0.1 broadcast_maximum_fusion
  43.7 0.0 copy-start.1
  43.7 9.3 %fusion = f32[4,8,128]{2,1,0:T(8,128)S(1)} fusion(f32[4,1024,128,8]{2,1,3,0:T(8,128)} %get-tuple-element.12, f32[4,8,128]{2,1,0:T(8,128)S(1)} %broadcast_maximum_fusion, pred[128,1024]{0,1:T(8,128)(4,1)S(1)} %iota_compare_fusion), kind=kLoop, calls=%fused_computation.5 | loop fusion | flops 16773120 | bytes 16941056 | tf_op jit(solution)/shard_map/reduce_sum | solution.py:71
  53.0 0.1 multiply_bitcast_fusion
  53.1 0.0 copy-done.1
  53.1 7.8 %divide_convert_fusion = bf16[128,4,8,64]{0,3,2,1:T(8,128)(2,1)S(1)} fusion(f32[4,1024,128,8]{2,1,3,0:T(8,128)} %get-tuple-element.12, f32[4,8,128]{2,1,0:T(8,128)S(1)} %broadcast_maximum_fusion, pred[128,1024]{0,1:T(8,128)(4,1)S(1)} %iota_compare_fusion, bf16[1024,4,2,64]{0,3,2,1:T(8,128)(2,1)S(1)} %bitcast.81, f32[128,4,8]{0,2,1:T(8,128)S(1)} %get-tuple-element.10, ...), kind=kOutput, calls=%fused_computation.22 | convolution fusion | flops 554434560 | bytes 18006016 | tf_op jit(solution)/shard_map/grtn,ngd->grtd/dot_general | solution.py:72
  60.9 0.0 copy-start
  60.9 7.1 %convolution_convert_fusion.1 = bf16[128,2880]{0,1:T(8,128)(2,1)} fusion(bf16[2048,2880]{0,1:T(8,128)(2,1)} %param.14, bf16[128,2048]{0,1:T(8,128)(2,1)S(1)} %bitcast.85), kind=kOutput, calls=%fused_computation.12 | convolution fusion | flops 1510318080 | bytes 13058048 | tf_op jit(solution)/shard_map/dot_general | solution.py:89
  68.0 0.0 copy-start.2
  68.0 0.0 all-reduce.3.cloned.1.call-update
  68.0 0.0 reduce-scatter.4.cloned.1.call-start
  68.1 0.1 mul.93
  68.2 2.6 scatter_custom_fusion
  70.9 29.3 %all-reduce.3.cloned.1.call-done = bf16[128,2880]{0,1:T(8,128)(2,1)} async-done(((bf16[128,2880]{0,1:T(8,128)(2,1)}), bf16[128,2880]{0,1:T(8,128)(2,1)}) %all-reduce.3.cloned.1.call-update) | async-done | bytes 737296 | tf_op jit(solution)/shard_map/psum | solution.py:90
  100.2 0.0 copy-done
  100.2 2.6 convert_add_fusion
  102.8 0.0 copy-done.2
  102.8 1.6 multiply_convert_fusion
  104.4 0.3 copy.46
  104.7 0.1 concatenate.3.clone
  104.8 4.6 %gather_fusion = bf16[640,2880]{1,0:T(8,128)(2,1)} fusion(bf16[129,2880]{1,0:T(8,128)(2,1)S(1)} %concatenate.3.clone, s32[1024]{0:T(1024)S(1)} %pad_clamp_fusion.1), kind=kCustom, calls=%fused_computation | custom fusion | bytes 7375360 | tf_op jit(solution)/shard_map/gather | solution.py:97
  109.4 89.4 %all_to_all.10 = bf16[8,80,2880]{2,1,0:T(8,128)(2,1)S(1)} all-to-all(bf16[8,80,2880]{2,1,0:T(8,128)(2,1)} %bitcast.75), channel_id=1, replica_groups=mesh['groups'=2,'tok'=8,'head'=2,'pair'=1] {'tok'}, dimensions={0} | all-to-all | bytes 7372800 | tf_op jit(solution)/shard_map/all_to_all | solution.py:98
  198.8 9.5 %fusion.28 = f32[640,1440]{0,1:T(8,128)S(1)} fusion(bf16[640,2880]{1,0:T(8,128)(2,1)S(1)} %bitcast.77, bf16[2880,1440]{0,1:T(8,128)(2,1)} %bitcast.84), kind=kOutput, calls=%fused_computation.58 | convolution fusion | flops 5308416000 | bytes 15667200 | tf_op jit(solution)/shard_map/dot_general | solution.py:25
  208.3 0.5 fusion.8
  208.8 1.0 copy.37
  209.9 7.0 %convolution_convert_fusion = bf16[8,80,2880]{2,1,0:T(8,128)(2,1)} fusion(bf16[8,80,720]{2,1,0:T(8,128)(2,1)S(1)} %bitcast.79, bf16[1,720,2880]{2,1,0:T(8,128)(2,1)} %param.19), kind=kOutput, calls=%fused_computation.10 | convolution fusion | flops 2656051200 | bytes 8755200 | tf_op jit(solution)/shard_map/dot_general | solution.py:101
  216.9 8.1 %copy.42 = bf16[8,80,2880]{1,0,2:T(8,128)(2,1)} copy(bf16[8,80,2880]{2,1,0:T(8,128)(2,1)} %convolution_convert_fusion) | data formatting | bytes 7372800
  225.0 9.6 %reshape.137 = bf16[2880,640]{1,0:T(8,128)(2,1)} reshape(bf16[2880,8,80]{2,1,0:T(8,128)(2,1)} %bitcast.74) | data formatting | bytes 7372800
  234.6 0.0 reduce-scatter.4.cloned.1.call-update
  234.6 47.5 %reduce-scatter.4.cloned.1.call-done = bf16[1440,640]{1,0:T(8,128)(2,1)} async-done(((bf16[2880,640]{1,0:T(8,128)(2,1)}), bf16[1440,640]{1,0:T(8,128)(2,1)}) %reduce-scatter.4.cloned.1.call-update) | async-done | bytes 1843216
  282.1 4.8 %reshape.138 = bf16[1440,8,80]{2,1,0:T(8,128)(2,1)S(1)} reshape(bf16[1440,640]{1,0:T(8,128)(2,1)} %reduce-scatter.4.cloned.1.call-done) | data formatting | bytes 3686400
  286.9 0.0 copy-start.3
  286.9 3.5 copy.43
  290.5 4.6 %all-to-all-start.1 = ((bf16[8,80,1440]{2,1,0:T(8,128)(2,1)}), bf16[8,80,1440]{2,1,0:T(8,128)(2,1)S(1)}, u32[]{:S(2)}, u32[]{:S(2)}) async-start(bf16[8,80,1440]{2,1,0:T(8,128)(2,1)} %copy.43), calls=%async_computation.1 | async-start | bytes 3932160 | tf_op jit(solution)/shard_map/all_to_all | solution.py:107
  295.1 0.1 reshape.116
  295.2 0.0 copy-done.3
  295.2 0.1 copy.32
  295.3 46.0 %all-to-all-done.1 = bf16[8,80,1440]{2,1,0:T(8,128)(2,1)S(1)} async-done(((bf16[8,80,1440]{2,1,0:T(8,128)(2,1)}), bf16[8,80,1440]{2,1,0:T(8,128)(2,1)S(1)}, u32[]{:S(2)}, u32[]{:S(2)}) %all-to-all-start.1) | async-done | bytes 1843232 | tf_op jit(solution)/shard_map/all_to_all | solution.py:107
  341.3 3.0 gather_fusion.1
  344.2 2.9 reshape.133
  347.2 3.1 multiply_reduce_fusion
  350.2 1.4 copy.38
  351.6 1.9 add_convert_fusion
  (11 shorter events, 0.1 us)
Async XLA Ops:
  6.5 29.0 %all-gather.2.cloned.1.call-start = ((), (), s32[]{:S(2)}) async-start(), calls=%async_computation.3 | async-start | bytes 1179648 | tf_op jit(solution)/shard_map/all_gather | solution.py:54
  8.2 92.0 %all-reduce.3.cloned.1.call-start = ((), (), s32[]{:S(2)}) async-start(), calls=%async_computation.4 | async-start | bytes 1474560 | tf_op jit(solution)/shard_map/psum | solution.py:90
  43.7 9.3 %copy-start.1 = (bf16[1024,512]{0,1:T(8,128)(2,1)S(1)}, bf16[1024,512]{0,1:T(8,128)(2,1)}, u32[]{:S(2)}) copy-start(bf16[1024,512]{0,1:T(8,128)(2,1)} %all-gather.2.cloned.1.call-done) | copy-start | bytes 3145732
  60.9 39.3 %copy-start = (bf16[128,2880]{0,1:T(8,128)(2,1)S(1)}, bf16[128,2880]{0,1:T(8,128)(2,1)}, u32[]{:S(2)}) copy-start(bf16[128,2880]{0,1:T(8,128)(2,1)} %param.13) | copy-start | bytes 2211844
  68.0 34.8 %copy-start.2 = (f32[2880]{0:T(1024)S(1)}, f32[2880]{0:T(1024)}, u32[]{:S(2)}) copy-start(f32[2880]{0:T(1024)} %param.15) | copy-start | bytes 34564
  68.0 214.1 %reduce-scatter.4.cloned.1.call-start = ((), (), s32[]{:S(2)}) async-start(), calls=%async_computation.5 | async-start | bytes 5529600
  286.9 8.3 %copy-start.3 = (f32[128,4]{0,1:T(4,128)S(1)}, f32[128,4]{0,1:T(4,128)}, u32[]{:S(2)}) copy-start(f32[128,4]{0,1:T(4,128)} %param.17) | copy-start | bytes 6148
  290.5 50.8 %all-to-all-start.1 = ((bf16[8,80,1440]{2,1,0:T(8,128)(2,1)}), bf16[8,80,1440]{2,1,0:T(8,128)(2,1)S(1)}, u32[]{:S(2)}, u32[]{:S(2)}) async-start(bf16[8,80,1440]{2,1,0:T(8,128)(2,1)} %copy.43), calls=%async_computation.1 | async-start | bytes 3932160 | tf_op jit(solution)/shard_map/all_to_all | solution.py:107
Sparse Core Ops, SparseCore 0:
  8.9 26.5 all-gather.1
  68.1 32.0 all-reduce.2
  234.7 47.3 reduce-scatter.3
